TPU v7x, 256 devices: a whole 4x4x8 slice. The times are simulated.
256 devices in a mesh: dp: 32 (over z_hi, y, core), tensor: 8 (over z_lo, x).
Axes of the slice: x: 4, y: 4, z: 8 (z_hi: 4, z_lo: 2; z = z_hi * 2 + z_lo), core: 2. Of those that a mesh axis runs over, the one named last changes fastest.
Arguments:
- tokens: bfloat16 [8192, 2560], P('dp'), may hold values from -6 to 6
- target: bfloat16 [8192, 2560], P('dp'), may hold values from -6 to 6
- norm_gain: float32 [2560], replicated, may hold values from 0.25 to 1.75
- gate_weight: bfloat16 [2560, 7168], P('dp', 'tensor'), may hold values from -0.125 to 0.125
- up_weight: bfloat16 [2560, 7168], P('dp', 'tensor'), may hold values from -0.125 to 0.125
- down_weight: bfloat16 [7168, 2560], P('tensor', 'dp'), may hold values from -0.0625 to 0.0625
- tangent: bfloat16 [2560, 7168], P('dp', 'tensor'), may hold values from -0.125 to 0.125
- lengths: int32 [4], replicated, may hold values from 512 to 2048
- loss_scale: float32 [1], replicated, may hold values from 16 to 64
Outputs:
- hvp: float32 [2560, 7168], P('dp', 'tensor')
- rayleigh: float32 [1], replicated
All inputs are finite; a program needn't handle non-finite values.
Results may differ from a plain program's by a relative error of at most 0.017.
Values may be sent and summed in bfloat16 or wider, within the bound.
No kernel may reach another device: no remote copies, remote signals or barrier semaphores. Data moves between devices by JAX's collectives and lax.ppermute only.
A program may use at most 128 MiB of HBM per device.

v0:
```python
import jax
import jax.numpy as jnp
from jax import lax
from jax.sharding import Mesh
from jax.sharding import PartitionSpec as P

DP = ("dp_0", "dp_1", "dp_2")
TENSOR = ("tensor_0", "tensor_1")
DP_TENSOR = ("dp_0", "dp_1", "dp_2", "tensor_0", "tensor_1")


def in_one_piece(arrays, axis, dim, along):
    both = jnp.concatenate(arrays, axis=along)
    filled, at, outs = (lax.all_gather(both, axis, axis=dim, tiled=True), 0, [])
    for a in arrays:
        outs.append(lax.slice_in_dim(filled, at, at + a.shape[along], axis=along))
        at += a.shape[along]
    return tuple(outs)


def one_axis_at_a_time(value, axes):
    for axis in axes:
        value = lax.psum(value, axis)
    return value


def token_weights(first_pos, row_total, micro_len, lengths, loss_scale):
    position = first_pos + jnp.arange(row_total, dtype=jnp.int32)
    micro_id = position // micro_len
    offset = position - micro_id * micro_len
    onehot = micro_id[:, None] == jnp.arange(lengths.shape[0], dtype=jnp.int32)[None, :]
    live_len = jnp.sum(jnp.where(onehot, lengths[None, :], 0), axis=1)
    return jnp.where(
        offset < live_len, loss_scale[0] / live_len.astype(jnp.float32), jnp.float32(0.0)
    )


def shards(
    tokens, target, norm_gain, gate_weight, up_weight, down_weight, tangent, lengths, loss_scale
):
    row_count = tokens.shape[0]
    stream = tokens.astype(jnp.float32)
    mean_sq = jnp.mean(stream * stream, axis=-1, keepdims=True)
    normed = (stream * lax.rsqrt(mean_sq + 1e-06) * norm_gain[None, :]).astype(jnp.bfloat16)
    pieces = in_one_piece((gate_weight, up_weight, tangent), DP, 0, 1)
    columns = normed
    gate_pre, up_pre, gate_tan = tuple(
        (jnp.dot(columns, piece, preferred_element_type=jnp.float32) for piece in pieces)
    )
    sigma = jax.nn.sigmoid(gate_pre)
    slope = sigma * (1.0 + gate_pre * (1.0 - sigma))
    bend = sigma * (1.0 - sigma) * (2.0 + gate_pre * (1.0 - 2.0 * sigma))
    hidden = (gate_pre * sigma * up_pre).astype(jnp.bfloat16)
    hidden_tan = (slope * gate_tan * up_pre).astype(jnp.bfloat16)
    down_full = lax.all_gather(down_weight, DP, axis=1, tiled=True)
    stacked = jnp.dot(
        jnp.concatenate([hidden, hidden_tan], axis=0), down_full, preferred_element_type=jnp.float32
    )
    branch = stacked[:row_count]
    branch_tan = stacked[row_count:]
    micro_len = row_count * lax.axis_size(DP) // lengths.shape[0]
    first_row = lax.axis_index(DP) * row_count
    branch, branch_tan = (
        lax.psum(branch.astype(jnp.bfloat16), TENSOR).astype(jnp.float32),
        lax.psum(branch_tan.astype(jnp.bfloat16), TENSOR).astype(jnp.float32),
    )
    weight = token_weights(first_row, row_count, micro_len, lengths, loss_scale)
    output = stream + branch
    grad_out = (weight[:, None] * (output - target.astype(jnp.float32))).astype(jnp.bfloat16)
    grad_tan = (weight[:, None] * branch_tan).astype(jnp.bfloat16)
    grads = lax.dot_general(
        jnp.concatenate([grad_out, grad_tan], axis=0),
        down_full,
        (((1,), (1,)), ((), ())),
        preferred_element_type=jnp.float32,
    )
    grad_hid = grads[:row_count]
    hess_hid = grads[row_count:]
    hess_pre = (hess_hid * up_pre * slope + grad_hid * up_pre * bend * gate_tan).astype(
        jnp.bfloat16
    )
    tangent_f = tangent.astype(jnp.float32)
    tangent_sq = jnp.sum(tangent_f * tangent_f)
    curvature, squares = (
        one_axis_at_a_time(jnp.sum(gate_tan * hess_pre.astype(jnp.float32)), DP_TENSOR),
        one_axis_at_a_time(tangent_sq, DP_TENSOR),
    )
    columns = normed
    product = lax.dot_general(
        columns, hess_pre, (((0,), (0,)), ((), ())), preferred_element_type=jnp.float32
    )
    hvp = lax.psum_scatter(
        lax.optimization_barrier(product.astype(jnp.bfloat16))
        .astype(jnp.float32)
        .astype(jnp.bfloat16),
        DP,
        scatter_dimension=0,
        tiled=True,
    ).astype(jnp.float32)
    rayleigh = (curvature / squares).reshape(1)
    return (hvp, rayleigh)


def solution(mesh):
    torus = Mesh(
        mesh.devices.reshape(4, 4, 2, 2, 4), ("dp_0", "dp_1", "dp_2", "tensor_0", "tensor_1")
    )
    return jax.shard_map(
        shards,
        mesh=torus,
        in_specs=(
            P(DP, None),
            P(DP, None),
            P(),
            P(DP, TENSOR),
            P(DP, TENSOR),
            P(TENSOR, DP),
            P(DP, TENSOR),
            P(),
            P(),
        ),
        out_specs=(P(DP, TENSOR), P()),
        check_vma=False,
    )
```

profile of v0, /device:TPU:2, one launch (start us, length us, event | category | flops | bytes accessed | tf_op | source)
XLA Modules:
  0.0 400.0 jit_solution(3529880794193507350)
XLA Ops:
  7.2 0.0 copy-start
  7.2 0.0 copy-start.7
  7.2 0.0 all-gather.3.cloned.1.call-start
  7.2 1.9 pad_maximum_fusion
  9.2 0.0 all-gather.3.cloned.1.call-update
  9.2 0.0 all-gather.5.cloned.1.call-start
  9.2 0.7 all-gather.5.cloned.1.call-update
  9.9 0.0 all-reduce.8.cloned.1.call-start
  10.0 1.7 fusion.6
  11.7 97.1 %all-gather.3.cloned.1.call-done = bf16[2560,2688]{1,0:T(8,128)(2,1)} async-done(((bf16[80,2688]{1,0:T(8,128)(2,1)}), bf16[2560,2688]{1,0:T(8,128)(2,1)}) %all-gather.3.cloned.1.call-update) | async-done | bytes 13762576 | tf_op jit(solution)/shard_map/all_gather | solution.py:14
  108.7 0.0 copy-done
  108.7 0.0 copy-done.7
  108.7 3.9 fusion
  112.6 3.9 fusion.4
  116.5 0.0 copy-start.2
  116.5 0.9 copy-done.2
  117.4 5.0 %multiply_convert_fusion.2 = (bf16[256,896]{1,0:T(8,128)(2,1)S(1)}, bf16[256,896]{1,0:T(8,128)(2,1)S(1)}, f32[256,896]{1,0:T(8,128)}) fusion(f32[256,896]{1,0:T(8,128)S(1)} %fusion.4, f32[256,896]{1,0:T(8,128)S(1)} %fusion, bf16[2560,2688]{1,0:T(8,128)(2,1)} %all-gather.3.cloned.1.call-done, bf16[256,2560]{1,0:T(8,128)(2,1)S(1)} %copy-done, ...), kind=kOutput, calls=%fused_computation.39 | convolution fusion | flops 1180008448 | bytes 9579520 | tf_op jit(solution)/shard_map/dot_general | solution.py:48
  122.4 58.1 %all-gather.5.cloned.1.call-done = bf16[896,2560]{0,1:T(8,128)(2,1)} async-done(((bf16[896,80]{0,1:T(8,128)(2,1)}), bf16[896,2560]{0,1:T(8,128)(2,1)}) %all-gather.5.cloned.1.call-update) | async-done | bytes 4587536 | tf_op jit(solution)/shard_map/all_gather | solution.py:55
  180.5 5.8 %convolution_convert_fusion.1 = bf16[512,2560]{1,0:T(8,128)(2,1)S(1)} fusion(bf16[896,2560]{0,1:T(8,128)(2,1)} %all-gather.5.cloned.1.call-done, bf16[256,896]{1,0:T(8,128)(2,1)S(1)} %get-tuple-element.19, bf16[256,896]{1,0:T(8,128)(2,1)S(1)} %get-tuple-element.18), kind=kOutput, calls=%fused_computation.7 | convolution fusion | flops 2351955968 | bytes 8126464 | tf_op jit(solution)/shard_map/dot_general | solution.py:56
  186.3 1.7 fusion.34
  188.0 0.0 copy-start.6
  188.0 0.0 copy-start.1
  188.0 0.0 all-reduce.8.cloned.1.call-update
  188.0 0.0 reduce-scatter.2.cloned.1.call-start
  188.8 0.0 copy-done.6
  188.9 0.1 select_reduce_fusion
  189.0 86.6 %all-reduce.8.cloned.1.call-done = (bf16[256,2560]{1,0:T(8,128)(2,1)}, bf16[256,2560]{1,0:T(8,128)(2,1)}) async-done(((bf16[256,2560]{1,0:T(8,128)(2,1)}, bf16[256,2560]{1,0:T(8,128)(2,1)}), (bf16[256,2560]{1,0:T(8,128)(2,1)}, bf16[256,2560]{1,0:T(8,128)(2,1)})) %all-reduce.8.cloned.1.call-update) | async-done | bytes 2621456 | tf_op jit(solution)/shard_map/psum | solution.py:65
  275.5 0.0 copy-done.1
  275.5 2.5 fusion.11
  278.1 0.0 copy-start.3
  278.1 0.0 copy-start.4
  278.1 5.3 %fusion.12 = f32[512,896]{1,0:T(8,128)S(1)} fusion(bf16[896,2560]{0,1:T(8,128)(2,1)} %all-gather.5.cloned.1.call-done, bf16[256,2560]{1,0:T(8,128)(2,1)S(1)} %get-tuple-element.21, bf16[256,2560]{1,0:T(8,128)(2,1)S(1)} %get-tuple-element.20), kind=kOutput, calls=%fused_computation.17 | convolution fusion | flops 2354053120 | bytes 9043968 | tf_op jit(solution)/shard_map/dot_general | solution.py:71
  283.4 0.0 copy-start.8
  283.4 0.0 copy-done.3
  283.4 0.0 copy-done.4
  283.4 1.3 multiply_reduce_fusion
  284.7 0.0 copy-done.8
  284.7 3.7 convolution_convert_fusion
  288.5 0.0 reduce-scatter.2.cloned.1.call-update
  288.5 0.9 copy-done.5
  289.4 0.7 multiply_reduce_fusion.1
  290.0 12.9 %all-reduce.2 = (f32[]{:T(128)}, f32[]{:T(128)}) all-reduce(f32[]{:T(128)} %get-tuple-element.14, f32[]{:T(128)} %multiply_reduce_fusion.1), channel_id=1, replica_groups=mesh['dp_0'=4,'dp_1'=4,'dp_2'=2,'tensor_0'=2,'tensor_1'=4] {'dp_0'}, use_global_device_ids=true, to_apply=%region_6.7 | all-reduce | flops 2 | bytes 16 | tf_op jit(solution)/shard_map/psum | solution.py:23
  302.9 11.1 %all-reduce.1 = (f32[]{:T(128)}, f32[]{:T(128)}) all-reduce(f32[]{:T(128)} %get-tuple-element.6, f32[]{:T(128)} %get-tuple-element.7), channel_id=1, replica_groups=mesh['dp_0'=4,'dp_1'=4,'dp_2'=2,'tensor_0'=2,'tensor_1'=4] {'dp_1'}, use_global_device_ids=true, to_apply=%region_7.8 | all-reduce | flops 2 | bytes 16 | tf_op jit(solution)/shard_map/psum | solution.py:23
  314.0 3.1 all-reduce.4
  317.1 5.5 %all-reduce.3 = (f32[]{:T(128)}, f32[]{:T(128)}) all-reduce(f32[]{:T(128)} %get-tuple-element.10, f32[]{:T(128)} %get-tuple-element.11), channel_id=1, replica_groups=mesh['dp_0'=4,'dp_1'=4,'dp_2'=2,'tensor_0'=2,'tensor_1'=4] {'tensor_0'}, use_global_device_ids=true, to_apply=%region_9.10 | all-reduce | flops 2 | bytes 16 | tf_op jit(solution)/shard_map/psum | solution.py:23
  322.6 9.6 %all-reduce = (f32[]{:T(128)}, f32[]{:T(128)}) all-reduce(f32[]{:T(128)} %get-tuple-element.8, f32[]{:T(128)} %get-tuple-element.9), channel_id=1, replica_groups=mesh['dp_0'=4,'dp_1'=4,'dp_2'=2,'tensor_0'=2,'tensor_1'=4] {'tensor_1'}, use_global_device_ids=true, to_apply=%region_10.11 | all-reduce | flops 2 | bytes 16 | tf_op jit(solution)/shard_map/psum | solution.py:23
  333.5 57.2 %reduce-scatter.2.cloned.1.call-done = bf16[80,896]{1,0:T(8,128)(2,1)} async-done(((bf16[2560,896]{1,0:T(8,128)(2,1)}), bf16[80,896]{1,0:T(8,128)(2,1)}) %reduce-scatter.2.cloned.1.call-update) | async-done | bytes 143376 | tf_op jit(solution)/shard_map/reduce_scatter | solution.py:92
  390.7 1.6 convert_element_type.65
  (4 shorter events, 0.0 us)
Async XLA Ops:
  7.2 101.6 %copy-start = (bf16[256,2560]{1,0:T(8,128)(2,1)S(1)}, bf16[256,2560]{1,0:T(8,128)(2,1)}, u32[]{:S(2)}) copy-start(bf16[256,2560]{1,0:T(8,128)(2,1)} %param.9) | copy-start | bytes 3932164
  7.2 101.6 %copy-start.7 = (f32[2560]{0:T(1024)S(1)}, f32[2560]{0:T(1024)}, u32[]{:S(2)}) copy-start(f32[2560]{0:T(1024)} %param.11) | copy-start | bytes 30724
  7.2 101.5 %all-gather.3.cloned.1.call-start = ((), (), s32[]{:S(2)}) async-start(), calls=%async_computation.1 | async-start | bytes 14192640 | tf_op jit(solution)/shard_map/all_gather | solution.py:14
  9.2 171.3 %all-gather.5.cloned.1.call-start = ((), (), s32[]{:S(2)}) async-start(), calls=%async_computation.2 | async-start | bytes 4730880 | tf_op jit(solution)/shard_map/all_gather | solution.py:55
  9.9 265.6 %all-reduce.8.cloned.1.call-start = ((), (), s32[]{:S(2)}) async-start(), calls=%async_computation.4 | async-start | bytes 5242880 | tf_op jit(solution)/shard_map/psum | solution.py:65
  116.5 0.9 copy-start.2
  188.0 0.8 copy-start.6
  188.0 87.5 %copy-start.1 = (bf16[256,2560]{1,0:T(8,128)(2,1)S(1)}, bf16[256,2560]{1,0:T(8,128)(2,1)}, u32[]{:S(2)}) copy-start(bf16[256,2560]{1,0:T(8,128)(2,1)} %param.10) | copy-start | bytes 3932164
  188.0 202.7 %reduce-scatter.2.cloned.1.call-start = ((), (), s32[]{:S(2)}) async-start(), calls=%async_computation.3 | async-start | bytes 4730880 | tf_op jit(solution)/shard_map/reduce_scatter | solution.py:92
  278.1 5.3 %copy-start.3 = (f32[256,896]{1,0:T(8,128)S(1)}, f32[256,896]{1,0:T(8,128)}, u32[]{:S(2)}) copy-start(f32[256,896]{1,0:T(8,128)} %copy-done.2) | copy-start | bytes 2752516
  278.1 5.3 %copy-start.4 = (f32[256,896]{1,0:T(8,128)S(1)}, f32[256,896]{1,0:T(8,128)}, u32[]{:S(2)}) copy-start(f32[256,896]{1,0:T(8,128)} %get-tuple-element.22) | copy-start | bytes 2752516
  283.4 1.3 copy-start.8
  288.4 0.9 copy-start.5
Sparse Core Ops, SparseCore 0:
  10.6 98.0 all-gather.2
  111.3 69.1 all-gather.4
  188.2 87.3 all-reduce.7
  288.6 102.0 reduce-scatter.1
where the time goes:
time: 401 us; the launch traced here: 400 us
  waiting for transfers between devices  300 us (75%)
  blocking collectives  42.1 us (10%)
  matrix products  27.5 us (7%)
  between operations  17.1 us (4%)
  other arithmetic  9.85 us (2%)
    all_gather x1, waiting for transfers between devices, in_one_piece(): filled, at, outs = (lax.all_gather(both, axis, axis=dim, tiled=True), 0, [])  97.1 us
    psum x1, waiting for transfers between devices, shards(): lax.psum(branch_tan.astype(jnp.bfloat16), TENSOR).astype(jnp.float32)  86.6 us
    all_gather x1, waiting for transfers between devices, shards(): down_full = lax.all_gather(down_weight, DP, axis=1, tiled=True)  58.1 us
    reduce_scatter x1, waiting for transfers between devices, shards(): lax.psum_scatter(lax.optimization_barrier(product.astype(jnp.bfloat16)).a...  57.2 us
    psum x5, blocking collectives, one_axis_at_a_time(): value = lax.psum(value, axis)  42.1 us
    dot_general x3, matrix products, shards(): jnp.dot(columns, piece, preferred_element_type=jnp.float32)  12.7 us
  transfers between devices with their start and end apart: 4, of which 4 were waited for; matrix products, arithmetic and copies ran while one was open for 4% of the time, Pallas kernels for 0%

commit v1 on v0

--- a/solution.py
+++ b/solution.py
@@ -52,7 +52,9 @@
     bend = sigma * (1.0 - sigma) * (2.0 + gate_pre * (1.0 - 2.0 * sigma))
     hidden = (gate_pre * sigma * up_pre).astype(jnp.bfloat16)
     hidden_tan = (slope * gate_tan * up_pre).astype(jnp.bfloat16)
-    down_full = lax.all_gather(down_weight, DP, axis=1, tiled=True)
+    down_full = jnp.concatenate(
+        lax.all_to_all(jnp.stack([down_weight] * lax.axis_size(DP)), DP, 0, 0), axis=1
+    )
     stacked = jnp.dot(
         jnp.concatenate([hidden, hidden_tan], axis=0), down_full, preferred_element_type=jnp.float32
     )

time: 401 us -> 435 us (1.085)
  waiting for transfers between devices: 300 us -> 320 us
  starting transfers between devices: 0.16 us -> 12 us
    all_gather x1, waiting for transfers between devices: 97.1 us -> 174 us  [in_one_piece(): filled, at, outs = (lax.all_gather(both, axis, axis=dim, tiled=True), 0, [])]
    all_gather x1 -> x0, waiting for transfers between devices: 58.1 us -> none  [shards(): down_full = lax.all_gather(down_weight, DP, axis=1, tiled=True)]
    all_to_all x0 -> x1, starting transfers between devices: none -> 11.7 us  [shards(): lax.all_to_all(jnp.stack([down_weight] * lax.axis_size(DP)), DP, 0, 0)]
  transfers between devices with their start and end apart: 4 -> 4, of which waited for: 4 -> 3; matrix products, arithmetic and copies ran while one was open for 4% -> 4% of each run, Pallas kernels for 0% -> 0%
where the time goes in v1:
time: 435 us; the launch traced here: 434 us
  waiting for transfers between devices  320 us (74%)
  blocking collectives  42.1 us (10%)
  matrix products  27.5 us (6%)
  between operations  17.1 us (4%)
  starting transfers between devices  12 us (3%)
  other arithmetic  8.46 us (2%)
  local copies, waits for them, and re-layouts  6.91 us (2%)
    all_gather x1, waiting for transfers between devices, in_one_piece(): filled, at, outs = (lax.all_gather(both, axis, axis=dim, tiled=True), 0, [])  174 us
    psum x1, waiting for transfers between devices, shards(): lax.psum(branch_tan.astype(jnp.bfloat16), TENSOR).astype(jnp.float32)  88.6 us
    reduce_scatter x1, waiting for transfers between devices, shards(): lax.psum_scatter(lax.optimization_barrier(product.astype(jnp.bfloat16)).a...  57.1 us
    psum x5, blocking collectives, one_axis_at_a_time(): value = lax.psum(value, axis)  42.1 us
    dot_general x3, matrix products, shards(): jnp.dot(columns, piece, preferred_element_type=jnp.float32)  12.7 us
    all_to_all x1, starting transfers between devices, shards(): lax.all_to_all(jnp.stack([down_weight] * lax.axis_size(DP)), DP, 0, 0)  11.7 us
  transfers between devices with their start and end apart: 4, of which 3 were waited for; matrix products, arithmetic and copies ran while one was open for 4% of the time, Pallas kernels for 0%

profile of v1, /device:TPU:2, one launch (start us, length us, event | category | flops | bytes accessed | tf_op | source)
XLA Modules:
  0.0 434.2 jit_solution(2164365283169006555)
XLA Ops:
  7.2 0.0 all-gather.2.cloned.1.call-start
  7.2 1.9 pad_maximum_fusion
  9.1 0.0 all-gather.2.cloned.1.call-update
  9.1 3.4 stack.2
  12.5 0.0 copy-start
  12.5 0.0 copy-start.7
  12.5 11.7 %all-to-all-start = ((bf16[32,896,80]{1,2,0:T(8,128)(2,1)}), bf16[32,896,80]{1,2,0:T(8,128)(2,1)}, u32[]{:S(2)}, u32[]{:S(2)}) async-start(bf16[32,896,80]{1,2,0:T(8,128)(2,1)} %stack.2), calls=%async_computation | async-start | bytes 9175040 | tf_op jit(solution)/shard_map/all_to_all | solution.py:56
  24.2 0.0 all-reduce.8.cloned.1.call-start
  24.3 0.0 copy-done
  24.3 0.3 fusion.6
  24.6 174.1 %all-gather.2.cloned.1.call-done = bf16[2560,2688]{1,0:T(8,128)(2,1)} async-done(((bf16[80,2688]{1,0:T(8,128)(2,1)}), bf16[2560,2688]{1,0:T(8,128)(2,1)}) %all-gather.2.cloned.1.call-update) | async-done | bytes 13762576 | tf_op jit(solution)/shard_map/all_gather | solution.py:14
  198.8 0.0 copy-done.7
  198.8 3.9 fusion
  202.7 3.9 fusion.4
  206.5 0.0 copy-start.2
  206.6 0.9 copy-done.2
  207.5 4.9 %multiply_convert_fusion.2 = (bf16[256,896]{1,0:T(8,128)(2,1)S(1)}, bf16[256,896]{1,0:T(8,128)(2,1)S(1)}, f32[256,896]{1,0:T(8,128)}) fusion(f32[256,896]{1,0:T(8,128)S(1)} %fusion.4, f32[256,896]{1,0:T(8,128)S(1)} %fusion, bf16[2560,2688]{1,0:T(8,128)(2,1)} %all-gather.2.cloned.1.call-done, bf16[256,2560]{1,0:T(8,128)(2,1)S(1)} %copy-done, ...), kind=kOutput, calls=%fused_computation.39 | convolution fusion | flops 1180008448 | bytes 9579520 | tf_op jit(solution)/shard_map/dot_general | solution.py:48
  212.4 0.0 all-to-all-done
  212.4 5.8 %convolution_convert_fusion.1 = bf16[512,2560]{1,0:T(8,128)(2,1)S(1)} fusion(bf16[896,2560]{0,1:T(8,128)(2,1)} %bitcast.2, bf16[256,896]{1,0:T(8,128)(2,1)S(1)} %get-tuple-element.19, bf16[256,896]{1,0:T(8,128)(2,1)S(1)} %get-tuple-element.18), kind=kOutput, calls=%fused_computation.7 | convolution fusion | flops 2351955968 | bytes 8126464 | tf_op jit(solution)/shard_map/dot_general | solution.py:58
  218.2 1.7 fusion.34
  219.9 0.0 copy-start.6
  219.9 0.0 copy-start.1
  219.9 0.0 all-reduce.8.cloned.1.call-update
  220.0 0.2 reduce-scatter.2.cloned.1.call-start
  221.0 0.0 copy-done.6
  221.0 0.1 select_reduce_fusion
  221.1 88.6 %all-reduce.8.cloned.1.call-done = (bf16[256,2560]{1,0:T(8,128)(2,1)}, bf16[256,2560]{1,0:T(8,128)(2,1)}) async-done(((bf16[256,2560]{1,0:T(8,128)(2,1)}, bf16[256,2560]{1,0:T(8,128)(2,1)}), (bf16[256,2560]{1,0:T(8,128)(2,1)}, bf16[256,2560]{1,0:T(8,128)(2,1)})) %all-reduce.8.cloned.1.call-update) | async-done | bytes 2621456 | tf_op jit(solution)/shard_map/psum | solution.py:67
  309.8 0.0 copy-done.1
  309.8 2.5 fusion.11
  312.3 0.0 copy-start.3
  312.3 0.0 copy-start.4
  312.3 5.3 %fusion.12 = f32[512,896]{1,0:T(8,128)S(1)} fusion(bf16[896,2560]{0,1:T(8,128)(2,1)} %bitcast.2, bf16[256,2560]{1,0:T(8,128)(2,1)S(1)} %get-tuple-element.21, bf16[256,2560]{1,0:T(8,128)(2,1)S(1)} %get-tuple-element.20), kind=kOutput, calls=%fused_computation.17 | convolution fusion | flops 2354053120 | bytes 9043968 | tf_op jit(solution)/shard_map/dot_general | solution.py:73
  317.6 0.0 copy-start.8
  317.6 0.0 copy-done.3
  317.6 0.0 copy-done.4
  317.6 1.3 multiply_reduce_fusion
  318.9 0.0 copy-done.8
  318.9 3.7 convolution_convert_fusion
  322.7 0.0 reduce-scatter.2.cloned.1.call-update
  322.7 0.9 copy-done.5
  323.6 0.7 multiply_reduce_fusion.1
  324.3 12.9 %all-reduce.2 = (f32[]{:T(128)}, f32[]{:T(128)}) all-reduce(f32[]{:T(128)} %get-tuple-element.14, f32[]{:T(128)} %multiply_reduce_fusion.1), channel_id=1, replica_groups=mesh['dp_0'=4,'dp_1'=4,'dp_2'=2,'tensor_0'=2,'tensor_1'=4] {'dp_0'}, use_global_device_ids=true, to_apply=%region_6.7 | all-reduce | flops 2 | bytes 16 | tf_op jit(solution)/shard_map/psum | solution.py:23
  337.1 11.1 %all-reduce.1 = (f32[]{:T(128)}, f32[]{:T(128)}) all-reduce(f32[]{:T(128)} %get-tuple-element.6, f32[]{:T(128)} %get-tuple-element.7), channel_id=1, replica_groups=mesh['dp_0'=4,'dp_1'=4,'dp_2'=2,'tensor_0'=2,'tensor_1'=4] {'dp_1'}, use_global_device_ids=true, to_apply=%region_7.8 | all-reduce | flops 2 | bytes 16 | tf_op jit(solution)/shard_map/psum | solution.py:23
  348.2 3.1 all-reduce.4
  351.3 5.5 %all-reduce.3 = (f32[]{:T(128)}, f32[]{:T(128)}) all-reduce(f32[]{:T(128)} %get-tuple-element.10, f32[]{:T(128)} %get-tuple-element.11), channel_id=1, replica_groups=mesh['dp_0'=4,'dp_1'=4,'dp_2'=2,'tensor_0'=2,'tensor_1'=4] {'tensor_0'}, use_global_device_ids=true, to_apply=%region_9.10 | all-reduce | flops 2 | bytes 16 | tf_op jit(solution)/shard_map/psum | solution.py:23
  356.8 9.5 %all-reduce = (f32[]{:T(128)}, f32[]{:T(128)}) all-reduce(f32[]{:T(128)} %get-tuple-element.8, f32[]{:T(128)} %get-tuple-element.9), channel_id=1, replica_groups=mesh['dp_0'=4,'dp_1'=4,'dp_2'=2,'tensor_0'=2,'tensor_1'=4] {'tensor_1'}, use_global_device_ids=true, to_apply=%region_10.11 | all-reduce | flops 2 | bytes 16 | tf_op jit(solution)/shard_map/psum | solution.py:23
  367.7 57.1 %reduce-scatter.2.cloned.1.call-done = bf16[80,896]{1,0:T(8,128)(2,1)} async-done(((bf16[2560,896]{1,0:T(8,128)(2,1)}), bf16[80,896]{1,0:T(8,128)(2,1)}) %reduce-scatter.2.cloned.1.call-update) | async-done | bytes 143376 | tf_op jit(solution)/shard_map/reduce_scatter | solution.py:94
  424.9 1.6 convert_element_type.65
  (4 shorter events, 0.0 us)
Async XLA Ops:
  7.2 191.6 %all-gather.2.cloned.1.call-start = ((), (), s32[]{:S(2)}) async-start(), calls=%async_computation.2 | async-start | bytes 14192640 | tf_op jit(solution)/shard_map/all_gather | solution.py:14
  12.5 11.8 %copy-start = (bf16[256,2560]{1,0:T(8,128)(2,1)S(1)}, bf16[256,2560]{1,0:T(8,128)(2,1)}, u32[]{:S(2)}) copy-start(bf16[256,2560]{1,0:T(8,128)(2,1)} %param.9) | copy-start | bytes 3932164
  12.5 186.3 %copy-start.7 = (f32[2560]{0:T(1024)S(1)}, f32[2560]{0:T(1024)}, u32[]{:S(2)}) copy-start(f32[2560]{0:T(1024)} %param.11) | copy-start | bytes 30724
  12.5 199.9 %all-to-all-start = ((bf16[32,896,80]{1,2,0:T(8,128)(2,1)}), bf16[32,896,80]{1,2,0:T(8,128)(2,1)}, u32[]{:S(2)}, u32[]{:S(2)}) async-start(bf16[32,896,80]{1,2,0:T(8,128)(2,1)} %stack.2), calls=%async_computation | async-start | bytes 9175040 | tf_op jit(solution)/shard_map/all_to_all | solution.py:56
  24.2 285.5 %all-reduce.8.cloned.1.call-start = ((), (), s32[]{:S(2)}) async-start(), calls=%async_computation.4 | async-start | bytes 5242880 | tf_op jit(solution)/shard_map/psum | solution.py:67
  206.5 0.9 copy-start.2
  219.9 1.1 copy-start.6
  219.9 89.8 %copy-start.1 = (bf16[256,2560]{1,0:T(8,128)(2,1)S(1)}, bf16[256,2560]{1,0:T(8,128)(2,1)}, u32[]{:S(2)}) copy-start(bf16[256,2560]{1,0:T(8,128)(2,1)} %param.10) | copy-start | bytes 3932164
  220.0 204.9 %reduce-scatter.2.cloned.1.call-start = ((), (), s32[]{:S(2)}) async-start(), calls=%async_computation.3 | async-start | bytes 4730880 | tf_op jit(solution)/shard_map/reduce_scatter | solution.py:94
  312.3 5.3 %copy-start.3 = (f32[256,896]{1,0:T(8,128)S(1)}, f32[256,896]{1,0:T(8,128)}, u32[]{:S(2)}) copy-start(f32[256,896]{1,0:T(8,128)} %copy-done.2) | copy-start | bytes 2752516
  312.3 5.3 %copy-start.4 = (f32[256,896]{1,0:T(8,128)S(1)}, f32[256,896]{1,0:T(8,128)}, u32[]{:S(2)}) copy-start(f32[256,896]{1,0:T(8,128)} %get-tuple-element.22) | copy-start | bytes 2752516
  317.6 1.3 copy-start.8
  322.7 0.9 copy-start.5
Sparse Core Ops, SparseCore 0:
  10.6 188.1 all-gather.1
  220.1 89.6 all-reduce.7
  322.8 101.9 reduce-scatter.1
